TPU v7x, 256 devices: a whole 4x4x8 slice. The times are simulated.
256 devices in a mesh: section: 8 (over x, core), ep: 32 (over y, z).
Axes of the slice: x: 4, y: 4, z: 8, core: 2. Of those that a mesh axis runs over, the one named last changes fastest.
Arguments:
- hidden_states: bfloat16 [1536, 6144], P('ep'), may hold values from -6 to 6
- route_experts: int32 [1536, 2], P('ep'), may hold values from 0 to 7, all different within a row; in each aligned block of 48 rows (0 to 47, 48 to 95, ...) at most 24 rows name the same one
- route_weights: float32 [1536, 2], P('ep'), may hold values from 0.05 to 1
- gate_weight: bfloat16 [32, 6144, 2048], P('ep', None, 'section'), may hold values from -0.078125 to 0.078125
- up_weight: bfloat16 [32, 6144, 2048], P('ep', None, 'section'), may hold values from -0.078125 to 0.078125
- down_weight: bfloat16 [32, 2048, 6144], P('ep', 'section'), may hold values from -0.0625 to 0.0625
Outputs:
- layer_out: bfloat16 [1536, 6144], P('ep', 'section')
Inputs may be any that keep to these rules, and one draw needn't show every extreme that they name: `route_experts`: each row names two different experts. Among the 48 rows of one ep index no expert is named by more than 24 rows, and in every draw some expert is named by exactly 24 rows of some ep index.
All inputs are finite; a program needn't handle non-finite values.
Results may differ from a plain program's by a relative error of at most 0.015.
Values may be sent and summed in bfloat16 or wider, within the bound.
A program may use at most 128 MiB of HBM per device.

v0:
```python
import jax
import jax.numpy as jnp
from jax import lax
from jax.sharding import PartitionSpec as P

EXPERTS = 8


def cut_along(x, dim, peers):
    before, after = (x.shape[:dim], x.shape[dim + 1 :])
    return jnp.moveaxis(x.reshape(*before, peers, -1, *after), dim, 0)


def sent_and_summed(x, axis, dim):
    peers = lax.axis_size(axis)
    parts = lax.all_to_all(cut_along(x, dim, peers), axis, 0, 0, tiled=True)
    return jnp.sum(parts.astype(jnp.float32), axis=0)


def expert_rows(incoming, gate_weight, up_weight, down_weight):
    sources, slot_count, features = incoming.shape
    stacked = incoming.reshape(sources * slot_count, features)
    gate_value = jnp.dot(stacked, gate_weight[0], preferred_element_type=jnp.float32)
    up_value = jnp.dot(stacked, up_weight[0], preferred_element_type=jnp.float32)
    hidden = (jax.nn.silu(gate_value) * up_value).astype(jnp.bfloat16)
    result = jnp.dot(hidden, down_weight[0], preferred_element_type=jnp.float32).astype(
        jnp.bfloat16
    )
    return result.reshape(sources, slot_count, features)


def on_device(hidden_states, route_experts, route_weights, gate_weight, up_weight, down_weight):
    ep_count = lax.axis_size("ep")
    section_count = lax.axis_size("section")
    tok_rows, features = hidden_states.shape
    members = ep_count // EXPERTS
    capacity = tok_rows // 2
    chosen = route_experts.reshape(-1)
    one_hot = (chosen[:, None] == jnp.arange(EXPERTS, dtype=jnp.int32)[None, :]).astype(jnp.int32)
    earlier = jnp.cumsum(one_hot, axis=0) - one_hot
    slot_index = jnp.sum(earlier * one_hot, axis=1)
    position = (chosen * capacity + slot_index).reshape(tok_rows, 2)
    columns = jnp.arange(EXPERTS * capacity, dtype=jnp.int32)
    matches = position[:, :, None] == columns[None, None, :]
    select = jnp.sum(matches.astype(jnp.int32), axis=1).astype(jnp.bfloat16)
    weighing = jnp.sum(matches.astype(jnp.float32) * route_weights[:, :, None], axis=1)
    packed = jnp.einsum(
        "tj,td->jd", select, hidden_states, preferred_element_type=jnp.float32
    ).astype(jnp.bfloat16)
    outgoing = jnp.repeat(packed.reshape(EXPERTS, capacity, features), members, axis=0)
    slot_share = capacity // section_count
    first_slot = lax.axis_index("section") * slot_share
    own_slots = lax.dynamic_slice_in_dim(outgoing, first_slot, slot_share, 1)
    arrived = lax.all_to_all(own_slots, "ep", split_axis=0, concat_axis=0, tiled=True)
    partials = expert_rows(
        lax.all_gather(arrived, "section", axis=1, tiled=True), gate_weight, up_weight, down_weight
    )
    summed = lax.psum_scatter(
        partials.astype(jnp.float32).astype(jnp.bfloat16),
        "section",
        scatter_dimension=1,
        tiled=True,
    ).astype(jnp.float32)
    returned = lax.all_to_all(
        summed.astype(jnp.bfloat16), "ep", split_axis=0, concat_axis=0, tiled=True
    ).astype(summed.dtype)
    merged = jnp.sum(returned.reshape(EXPERTS, members, slot_share, features), axis=1)
    weigh_part = lax.dynamic_slice_in_dim(
        weighing.reshape(tok_rows, EXPERTS, capacity), first_slot, slot_share, 2
    )
    contribution = jnp.dot(
        weigh_part.reshape(tok_rows, EXPERTS * slot_share),
        merged.reshape(EXPERTS * slot_share, features),
        preferred_element_type=jnp.float32,
    )
    layer_out = sent_and_summed(contribution.astype(jnp.bfloat16), "section", 1)
    return layer_out.astype(jnp.bfloat16)


def solution(mesh):
    return jax.shard_map(
        on_device,
        mesh=mesh,
        in_specs=(
            P("ep", None),
            P("ep", None),
            P("ep", None),
            P("ep", None, "section"),
            P("ep", None, "section"),
            P("ep", "section", None),
        ),
        out_specs=P("ep", "section"),
        check_vma=False,
    )
```

profile of v0, /device:TPU:1, one launch (start us, length us, event | category | flops | bytes accessed | tf_op | source)
XLA Modules:
  0.0 317.6 jit_solution(11855568616730549436)
XLA Ops:
  6.5 0.0 copy-start
  6.5 0.0 all-gather.2.cloned.1.call-start
  6.5 0.9 copy.60
  7.5 0.1 eq.28
  7.6 0.1 fusion.21
  7.7 0.1 reduce_window_sum.11
  7.8 0.2 select_reduce_fusion.1
  8.0 0.1 reduce_sum.51
  8.1 0.1 copy.61
  8.2 0.7 multiply_add_fusion
  8.9 0.1 convert_reduce_fusion.1
  9.0 1.9 convolution_convert_fusion.1
  10.8 4.8 %broadcast_in_dim.2 = bf16[8,4,24,6144]{3,2,1,0:T(8,128)(2,1)} broadcast(bf16[8,24,6144]{2,1,0:T(8,128)(2,1)S(1)} %bitcast.41), dimensions={0,2,3} | broadcast | bytes 11796480 | tf_op jit(solution)/shard_map/broadcast_in_dim | solution.py:50
  15.6 4.0 %constant_dynamic-slice_fusion.1 = bf16[32,3,6144]{2,1,0:T(4,128)(2,1)S(1)} fusion(bf16[32,24,6144]{2,1,0:T(8,128)(2,1)} %bitcast.37, s32[]{:T(128)S(6)} %select_n.4), kind=kLoop, calls=%fused_computation.30 | loop fusion | bytes 2359300 | tf_op jit(solution)/shard_map/dynamic_slice | solution.py:53
  19.6 48.3 %all_to_all.15 = bf16[32,3,6144]{2,1,0:T(4,128)(2,1)S(1)} all-to-all(bf16[32,3,6144]{2,1,0:T(4,128)(2,1)S(1)} %constant_dynamic-slice_fusion.1), channel_id=1, replica_groups=mesh['section'=8,'ep'=32] {'ep'}, dimensions={0} | all-to-all | bytes 2359296 | tf_op jit(solution)/shard_map/all_to_all | solution.py:54
  67.9 1.9 copy.64
  69.8 0.0 all-gather.2.cloned.1.call-update
  69.8 0.2 reduce-scatter.2.cloned.1.call-start
  70.0 57.2 %all-gather.2.cloned.1.call-done = bf16[32,24,6144]{2,0,1:T(8,128)(2,1)} async-done(((bf16[32,3,6144]{2,0,1:T(8,128)(2,1)}), bf16[32,24,6144]{2,0,1:T(8,128)(2,1)}) %all-gather.2.cloned.1.call-update) | async-done | bytes 9437200 | tf_op jit(solution)/shard_map/all_gather | solution.py:56
  127.2 12.5 %copy.65 = bf16[32,24,6144]{2,1,0:T(8,128)(2,1)} copy(bf16[32,24,6144]{2,0,1:T(8,128)(2,1)} %all-gather.2.cloned.1.call-done) | data formatting | bytes 18874368 | tf_op jit(solution)/shard_map/all_gather | solution.py:56
  139.7 8.1 %fusion.4 = f32[768,256]{1,0:T(8,128)} fusion(bf16[768,6144]{1,0:T(8,128)(2,1)} %bitcast.38, bf16[1,6144,256]{2,1,0:T(8,128)(2,1)} %param.9), kind=kOutput, calls=%fused_computation.8 | convolution fusion | flops 2415919104 | bytes 13369344 | tf_op jit(solution)/shard_map/dot_general | solution.py:23
  147.7 0.0 copy-done
  147.7 19.4 %convolution_convert_fusion = bf16[768,6144]{1,0:T(8,128)(2,1)} fusion(bf16[1,256,6144]{2,1,0:T(8,128)(2,1)S(1)} %copy-done, bf16[768,6144]{1,0:T(8,128)(2,1)} %bitcast.39, bf16[1,6144,256]{2,1,0:T(8,128)(2,1)} %param.10, f32[768,256]{1,0:T(8,128)} %fusion.4), kind=kOutput, calls=%fused_computation | convolution fusion | flops 4837736448 | bytes 25952256 | tf_op jit(solution)/shard_map/dot_general | solution.py:26
  167.1 12.5 %copy.66 = bf16[32,24,6144]{2,0,1:T(8,128)(2,1)} copy(bf16[32,24,6144]{2,1,0:T(8,128)(2,1)} %bitcast.40) | data formatting | bytes 18874368 | tf_op jit(solution)/shard_map/reshape | solution.py:29
  179.6 0.0 reduce-scatter.2.cloned.1.call-update
  179.6 0.0 copy-start.2
  179.7 59.5 %reduce-scatter.2.cloned.1.call-done = bf16[32,3,6144]{2,0,1:T(8,128)(2,1)} async-done(((bf16[32,24,6144]{2,0,1:T(8,128)(2,1)}), bf16[32,3,6144]{2,0,1:T(8,128)(2,1)}) %reduce-scatter.2.cloned.1.call-update) | async-done | bytes 1179664 | tf_op jit(solution)/shard_map/reduce_scatter | solution.py:58
  239.1 3.4 %copy.67 = bf16[32,3,6144]{2,1,0:T(4,128)(2,1)} copy(bf16[32,3,6144]{2,0,1:T(8,128)(2,1)} %reduce-scatter.2.cloned.1.call-done) | data formatting | bytes 2359296 | tf_op jit(solution)/shard_map/reduce_scatter | solution.py:58
  242.5 9.7 %all-to-all-start.1 = ((bf16[32,3,6144]{2,1,0:T(4,128)(2,1)}), bf16[32,3,6144]{2,1,0:T(4,128)(2,1)}, u32[]{:S(2)}, u32[]{:S(2)}) async-start(bf16[32,3,6144]{2,1,0:T(4,128)(2,1)} %copy.67), calls=%async_computation.2 | async-start | bytes 3145728 | tf_op jit(solution)/shard_map/all_to_all | solution.py:64
  252.2 0.0 copy-done.2
  252.2 0.0 copy-start.1
  252.3 0.1 select_reduce_fusion
  252.4 0.1 copy.62
  252.5 36.7 %all-to-all-done.1 = bf16[32,3,6144]{2,1,0:T(4,128)(2,1)} async-done(((bf16[32,3,6144]{2,1,0:T(4,128)(2,1)}), bf16[32,3,6144]{2,1,0:T(4,128)(2,1)}, u32[]{:S(2)}, u32[]{:S(2)}) %all-to-all-start.1) | async-done | bytes 1179680 | tf_op jit(solution)/shard_map/all_to_all | solution.py:64
  289.2 2.4 convert_reduce_fusion
  291.5 0.4 fusion
  292.0 17.0 %all_to_all.16 = bf16[8,48,768]{2,1,0:T(8,128)(2,1)} all-to-all(bf16[8,48,768]{2,1,0:T(8,128)(2,1)S(1)} %bitcast.43), channel_id=1, replica_groups=mesh['section'=8,'ep'=32] {'section'}, dimensions={0} | all-to-all | bytes 1179648 | tf_op jit(solution)/shard_map/all_to_all | solution.py:16
  308.9 1.8 reduce_sum.55
  310.7 0.0 copy-done.1
  (2 shorter events, 0.1 us)
Async XLA Ops:
  6.5 141.2 %copy-start = (bf16[1,256,6144]{2,1,0:T(8,128)(2,1)S(1)}, bf16[1,256,6144]{2,1,0:T(8,128)(2,1)}, u32[]{:S(2)}) copy-start(bf16[1,256,6144]{2,1,0:T(8,128)(2,1)} %param.11) | copy-start | bytes 9437188
  6.5 120.6 %all-gather.2.cloned.1.call-start = ((), (), s32[]{:S(2)}) async-start(), calls=%async_computation.4 | async-start | bytes 10616832 | tf_op jit(solution)/shard_map/all_gather | solution.py:56
  69.8 169.3 %reduce-scatter.2.cloned.1.call-start = ((), (), s32[]{:S(2)}) async-start(), calls=%async_computation.5 | async-start | bytes 10616832 | tf_op jit(solution)/shard_map/reduce_scatter | solution.py:58
  179.6 72.6 %copy-start.2 = (f32[48,2]{0,1:T(2,128)S(1)}, f32[48,2]{0,1:T(2,128)}, u32[]{:S(2)}) copy-start(f32[48,2]{0,1:T(2,128)} %param.8) | copy-start | bytes 1156
  242.5 46.6 %all-to-all-start.1 = ((bf16[32,3,6144]{2,1,0:T(4,128)(2,1)}), bf16[32,3,6144]{2,1,0:T(4,128)(2,1)}, u32[]{:S(2)}, u32[]{:S(2)}) async-start(bf16[32,3,6144]{2,1,0:T(4,128)(2,1)} %copy.67), calls=%async_computation.2 | async-start | bytes 3145728 | tf_op jit(solution)/shard_map/all_to_all | solution.py:64
  252.2 58.5 %copy-start.1 = (bf16[1,256,6144]{2,1,0:T(8,128)(2,1)S(1)}, bf16[1,256,6144]{2,1,0:T(8,128)(2,1)}, u32[]{:S(2)}) copy-start(bf16[1,256,6144]{2,1,0:T(8,128)(2,1)} %param.11) | copy-start | bytes 9437188
Sparse Core Ops, SparseCore 0:
  69.9 57.2 all-gather.1
  179.8 59.3 reduce-scatter.1
where the time goes:
time: 318 us
  waiting for transfers between devices  153 us (48%)
  blocking collectives  65.3 us (21%)
  local copies, waits for them, and re-layouts  40.4 us (13%)
  matrix products  29.7 us (9%)
  between operations  13.5 us (4%)
  starting transfers between devices  9.91 us (3%)
  other arithmetic  5.43 us (2%)
    reduce_scatter x1, waiting for transfers between devices, on_device(): lax.psum_scatter(partials.astype(jnp.float32).astype(jnp.bfloat16), 'sect...  59.5 us
    all_gather x1, waiting for transfers between devices, on_device(): lax.all_gather(arrived, 'section', axis=1, tiled=True)  57.2 us
    all_to_all x1, blocking collectives, on_device(): lax.all_to_all(own_slots, 'ep', split_axis=0, concat_axis=0, tiled=True)  48.3 us
    all_to_all x1, waiting for transfers between devices, on_device(): lax.all_to_all(summed.astype(jnp.bfloat16), 'ep', split_axis=0, concat_ax...  36.7 us
    dot_general x1, matrix products, expert_rows(): jnp.dot(hidden, down_weight[0], preferred_element_type=jnp.float32)  19.4 us
    all_to_all x1, blocking collectives, sent_and_summed(): parts = lax.all_to_all(cut_along(x, dim, peers), axis, 0, 0, tiled=True)  17 us
    reshape x1, local copies, waits for them, and re-layouts, expert_rows(): return result.reshape(sources, slot_count, features)  12.5 us
    all_gather x1, local copies, waits for them, and re-layouts, on_device(): lax.all_gather(arrived, 'section', axis=1, tiled=True)  12.5 us
  transfers between devices with their start and end apart: 3, of which 3 were waited for; matrix products, arithmetic and copies ran while one was open for 0% of the time, Pallas kernels for 0%

commit v1 on v0

--- a/solution.py
+++ b/solution.py
@@ -4,6 +4,22 @@
 from jax.sharding import PartitionSpec as P
 
 EXPERTS = 8
+
+
+def gather_around(x, axis, dim):
+    ways, here, hop = (lax.axis_size(axis), lax.axis_index(axis), x.shape[dim])
+    shape = [n * ways if d == dim else n for d, n in enumerate(x.shape)]
+    full = lax.dynamic_update_slice_in_dim(jnp.zeros(shape, x.dtype), x, here * hop, axis=dim)
+    going_up = going_down = x
+    for far in range(1, ways // 2 + 1):
+        going_up = lax.ppermute(going_up, axis, [(d, (d + 1) % ways) for d in range(ways)])
+        full = lax.dynamic_update_slice_in_dim(full, going_up, (here - far) % ways * hop, axis=dim)
+        if 2 * far < ways:
+            going_down = lax.ppermute(going_down, axis, [(d, (d - 1) % ways) for d in range(ways)])
+            full = lax.dynamic_update_slice_in_dim(
+                full, going_down, (here + far) % ways * hop, axis=dim
+            )
+    return full
 
 
 def cut_along(x, dim, peers):
@@ -53,7 +69,7 @@
     own_slots = lax.dynamic_slice_in_dim(outgoing, first_slot, slot_share, 1)
     arrived = lax.all_to_all(own_slots, "ep", split_axis=0, concat_axis=0, tiled=True)
     partials = expert_rows(
-        lax.all_gather(arrived, "section", axis=1, tiled=True), gate_weight, up_weight, down_weight
+        gather_around(arrived, "section", 1), gate_weight, up_weight, down_weight
     )
     summed = lax.psum_scatter(
         partials.astype(jnp.float32).astype(jnp.bfloat16),

time: 318 us -> 503 us (1.58)
  local copies, waits for them, and re-layouts: 40.4 us -> 228 us
  waiting for transfers between devices: 153 us -> 132 us
  starting transfers between devices: 9.91 us -> 23.4 us
    dynamic_update_slice x0 -> x8, local copies, waits for them, and re-layouts: none -> 170 us  [the longest x4 84.2 us: gather_around(): lax.dynamic_update_slice_in_dim(full, going_up, (here - far) % ways * hop...]
    all_gather x1 -> x0, waiting for transfers between devices: 57.2 us -> none  [on_device(): lax.all_gather(arrived, 'section', axis=1, tiled=True)]
    ppermute x0 -> x7, waiting for transfers between devices: none -> 37 us  [the longest x4 35.9 us: gather_around(): lax.ppermute(going_up, axis, [(d, (d + 1) % ways) for d in range(ways)])]
    ppermute x0 -> x7, local copies, waits for them, and re-layouts: none -> 24.1 us  [the longest x4 13.8 us: gather_around(): lax.ppermute(going_up, axis, [(d, (d + 1) % ways) for d in range(ways)])]
    ppermute x0 -> x7, starting transfers between devices: none -> 13.7 us  [the longest x4 12.4 us: gather_around(): lax.ppermute(going_up, axis, [(d, (d + 1) % ways) for d in range(ways)])]
    all_gather x1 -> x0, local copies, waits for them, and re-layouts: 12.5 us -> none  [on_device(): lax.all_gather(arrived, 'section', axis=1, tiled=True)]
  transfers between devices with their start and end apart: 3 -> 9, of which waited for: 3 -> 6; matrix products, arithmetic and copies ran while one was open for 0% -> 35% of each run, Pallas kernels for 0% -> 0%
where the time goes in v1:
time: 503 us; the launch traced here: 498 us
  local copies, waits for them, and re-layouts  228 us (45%)
  waiting for transfers between devices  132 us (26%)
  blocking collectives  65.3 us (13%)
  matrix products  29.7 us (6%)
  starting transfers between devices  23.4 us (5%)
  between operations  13.5 us (3%)
  other arithmetic  5.43 us (1%)
    dynamic_update_slice x4, local copies, waits for them, and re-layouts, gather_around(): lax.dynamic_update_slice_in_dim(full, going_up, (here - far) % ways * hop...  84.2 us
    dynamic_update_slice x3, local copies, waits for them, and re-layouts, gather_around(): lax.dynamic_update_slice_in_dim(full, going_down, (here + far) % ways * h...  64.5 us
    reduce_scatter x1, waiting for transfers between devices, on_device(): lax.psum_scatter(partials.astype(jnp.float32).astype(jnp.bfloat16), 'sect...  58.6 us
    all_to_all x1, blocking collectives, on_device(): lax.all_to_all(own_slots, 'ep', split_axis=0, concat_axis=0, tiled=True)  48.3 us
    all_to_all x1, waiting for transfers between devices, on_device(): lax.all_to_all(summed.astype(jnp.bfloat16), 'ep', split_axis=0, concat_ax...  36.7 us
    ppermute x4, waiting for transfers between devices, gather_around(): lax.ppermute(going_up, axis, [(d, (d + 1) % ways) for d in range(ways)])  35.9 us
    dynamic_update_slice x1, local copies, waits for them, and re-layouts, gather_around(): lax.dynamic_update_slice_in_dim(jnp.zeros(shape, x.dtype), x, here * hop,...  21.5 us
    dot_general x1, matrix products, expert_rows(): jnp.dot(hidden, down_weight[0], preferred_element_type=jnp.float32)  19.4 us
  transfers between devices with their start and end apart: 9, of which 6 were waited for; matrix products, arithmetic and copies ran while one was open for 35% of the time, Pallas kernels for 0%

profile of v1, /device:TPU:1, one launch (start us, length us, event | category | flops | bytes accessed | tf_op | source)
XLA Modules:
  0.0 498.0 jit_solution(6945314227604992000)
XLA Ops:
  6.5 0.9 copy.81
  7.7 0.1 reduce_window_sum.11
  7.8 0.2 select_reduce_fusion.1
  8.2 0.7 multiply_add_fusion
  9.0 1.9 convolution_convert_fusion.1
  10.8 4.8 broadcast_in_dim.10
  15.6 4.0 constant_dynamic-slice_fusion
  19.6 48.3 %all_to_all.15 = bf16[32,3,6144]{2,1,0:T(4,128)(2,1)S(1)} all-to-all(bf16[32,3,6144]{2,1,0:T(4,128)(2,1)S(1)} %constant_dynamic-slice_fusion), channel_id=1, replica_groups=mesh['section'=8,'ep'=32] {'ep'}, dimensions={0} | all-to-all | bytes 2359296 | tf_op jit(solution)/shard_map/all_to_all | solution.py:70
  67.9 1.2 copy-done.1
  69.1 0.9 copy.85
  69.9 4.8 collective-permute-start
  74.8 13.1 %collective-permute-done = bf16[32,3,6144]{2,0,1:T(8,128)(2,1)S(1)} collective-permute-done((bf16[32,3,6144]{2,0,1:T(8,128)(2,1)S(1)}, bf16[32,3,6144]{2,0,1:T(8,128)(2,1)S(1)}, u32[]{:S(2)}, u32[]{:S(2)}) %collective-permute-start) | collective-permute-done | bytes 1179680 | tf_op jit(solution)/shard_map/ppermute | solution.py:15
  87.9 2.5 collective-permute-start.2
  90.4 1.0 copy-done.2
  91.5 0.1 collective-permute-start.3
  91.6 11.9 %collective-permute-done.2 = bf16[32,3,6144]{2,0,1:T(8,128)(2,1)S(1)} collective-permute-done((bf16[32,3,6144]{2,0,1:T(8,128)(2,1)S(1)}, bf16[32,3,6144]{2,0,1:T(8,128)(2,1)S(1)}, u32[]{:S(2)}, u32[]{:S(2)}) %collective-permute-start.2) | collective-permute-done | bytes 1179680 | tf_op jit(solution)/shard_map/ppermute | solution.py:15
  103.6 2.5 collective-permute-start.4
  106.0 1.2 collective-permute-done.3
  107.2 1.2 collective-permute-start.5
  108.4 10.8 %collective-permute-done.4 = bf16[32,3,6144]{2,0,1:T(8,128)(2,1)} collective-permute-done((bf16[32,3,6144]{2,0,1:T(8,128)(2,1)S(1)}, bf16[32,3,6144]{2,0,1:T(8,128)(2,1)}, u32[]{:S(2)}, u32[]{:S(2)}) %collective-permute-start.4) | collective-permute-done | bytes 1179680 | tf_op jit(solution)/shard_map/ppermute | solution.py:15
  119.2 2.6 collective-permute-start.6
  121.8 4.8 broadcast_in_dim.4
  126.6 21.5 %dynamic_update_slice.24 = bf16[32,24,6144]{2,1,0:T(8,128)(2,1)} dynamic-update-slice(bf16[32,24,6144]{2,1,0:T(8,128)(2,1)} %broadcast_in_dim.4, bf16[32,3,6144]{2,1,0:T(4,128)(2,1)} %copy-done.1, s32[]{:T(128)} %constant.60.clone.1, s32[]{:T(128)S(6)} %select_n.57, s32[]{:T(128)} %constant.60.clone.1) | dynamic-update-slice | bytes 2359300 | tf_op jit(solution)/shard_map/dynamic_update_slice | solution.py:12
  148.1 3.5 copy.86
  151.5 21.5 %dynamic_update_slice.25 = bf16[32,24,6144]{2,1,0:T(8,128)(2,1)} dynamic-update-slice(bf16[32,24,6144]{2,1,0:T(8,128)(2,1)} %dynamic_update_slice.24, bf16[32,3,6144]{2,1,0:T(4,128)(2,1)} %copy.86, s32[]{:T(128)} %constant.60.clone.1, s32[]{:T(128)S(6)} %select_n.59, s32[]{:T(128)} %constant.60.clone.1) | dynamic-update-slice | bytes 2359300 | tf_op jit(solution)/shard_map/dynamic_update_slice | solution.py:16
  173.1 3.4 copy.88
  176.5 21.5 %dynamic_update_slice.26 = bf16[32,24,6144]{2,1,0:T(8,128)(2,1)} dynamic-update-slice(bf16[32,24,6144]{2,1,0:T(8,128)(2,1)} %dynamic_update_slice.25, bf16[32,3,6144]{2,1,0:T(4,128)(2,1)} %copy.88, s32[]{:T(128)} %constant.60.clone.1, s32[]{:T(128)S(6)} %select_n.61, s32[]{:T(128)} %constant.60.clone.1) | dynamic-update-slice | bytes 2359300 | tf_op jit(solution)/shard_map/dynamic_update_slice | solution.py:19
  198.0 3.4 copy.89
  201.4 20.6 %dynamic_update_slice.27 = bf16[32,24,6144]{2,1,0:T(8,128)(2,1)} dynamic-update-slice(bf16[32,24,6144]{2,1,0:T(8,128)(2,1)} %dynamic_update_slice.26, bf16[32,3,6144]{2,1,0:T(4,128)(2,1)} %copy.89, s32[]{:T(128)} %constant.60.clone.1, s32[]{:T(128)S(6)} %select_n.63, s32[]{:T(128)} %constant.60.clone.1) | dynamic-update-slice | bytes 2359300 | tf_op jit(solution)/shard_map/dynamic_update_slice | solution.py:16
  222.0 3.4 copy.90
  225.4 21.5 %dynamic_update_slice.28 = bf16[32,24,6144]{2,1,0:T(8,128)(2,1)} dynamic-update-slice(bf16[32,24,6144]{2,1,0:T(8,128)(2,1)} %dynamic_update_slice.27, bf16[32,3,6144]{2,1,0:T(4,128)(2,1)} %copy.90, s32[]{:T(128)} %constant.60.clone.1, s32[]{:T(128)S(6)} %select_n.65, s32[]{:T(128)} %constant.60.clone.1) | dynamic-update-slice | bytes 2359300 | tf_op jit(solution)/shard_map/dynamic_update_slice | solution.py:19
  247.0 3.4 copy.91
  250.4 20.6 %dynamic_update_slice.29 = bf16[32,24,6144]{2,1,0:T(8,128)(2,1)} dynamic-update-slice(bf16[32,24,6144]{2,1,0:T(8,128)(2,1)} %dynamic_update_slice.28, bf16[32,3,6144]{2,1,0:T(4,128)(2,1)} %copy.91, s32[]{:T(128)} %constant.60.clone.1, s32[]{:T(128)S(6)} %select_n.67, s32[]{:T(128)} %constant.60.clone.1) | dynamic-update-slice | bytes 2359300 | tf_op jit(solution)/shard_map/dynamic_update_slice | solution.py:16
  271.0 3.4 copy.92
  274.4 21.5 %dynamic_update_slice.30 = bf16[32,24,6144]{2,1,0:T(8,128)(2,1)} dynamic-update-slice(bf16[32,24,6144]{2,1,0:T(8,128)(2,1)} %dynamic_update_slice.29, bf16[32,3,6144]{2,1,0:T(4,128)(2,1)} %copy.92, s32[]{:T(128)} %constant.60.clone.1, s32[]{:T(128)S(6)} %select_n.69, s32[]{:T(128)} %constant.60.clone.1) | dynamic-update-slice | bytes 2359300 | tf_op jit(solution)/shard_map/dynamic_update_slice | solution.py:19
  295.9 3.5 copy.93
  299.4 21.5 %dynamic_update_slice.31 = bf16[32,24,6144]{2,1,0:T(8,128)(2,1)} dynamic-update-slice(bf16[32,24,6144]{2,1,0:T(8,128)(2,1)} %dynamic_update_slice.30, bf16[32,3,6144]{2,1,0:T(4,128)(2,1)} %copy.93, s32[]{:T(128)} %constant.60.clone.1, s32[]{:T(128)S(6)} %select_n.71, s32[]{:T(128)} %constant.60.clone.1) | dynamic-update-slice | bytes 2359300 | tf_op jit(solution)/shard_map/dynamic_update_slice | solution.py:16
  320.9 8.1 %fusion.2 = f32[768,256]{1,0:T(8,128)} fusion(bf16[768,6144]{1,0:T(8,128)(2,1)} %bitcast.37, bf16[1,6144,256]{2,1,0:T(8,128)(2,1)} %param.10), kind=kOutput, calls=%fused_computation.6 | convolution fusion | flops 2415919104 | bytes 13369344 | tf_op jit(solution)/shard_map/dot_general | solution.py:40
  329.0 19.4 %convolution_convert_fusion = bf16[768,6144]{1,0:T(8,128)(2,1)} fusion(bf16[1,256,6144]{2,1,0:T(8,128)(2,1)S(1)} %copy-done, f32[768,256]{1,0:T(8,128)} %fusion.2, bf16[768,6144]{1,0:T(8,128)(2,1)} %bitcast.38, bf16[1,6144,256]{2,1,0:T(8,128)(2,1)} %param.9), kind=kOutput, calls=%fused_computation | convolution fusion | flops 4837736448 | bytes 25952256 | tf_op jit(solution)/shard_map/dot_general | solution.py:42
  348.4 12.5 %copy.94 = bf16[32,24,6144]{2,0,1:T(8,128)(2,1)} copy(bf16[32,24,6144]{2,1,0:T(8,128)(2,1)} %bitcast.36) | data formatting | bytes 18874368 | tf_op jit(solution)/shard_map/reshape | solution.py:45
  360.9 58.6 %reduce-scatter.2.cloned.1.call-done = bf16[32,3,6144]{2,0,1:T(8,128)(2,1)} async-done(((bf16[32,24,6144]{2,0,1:T(8,128)(2,1)}), bf16[32,3,6144]{2,0,1:T(8,128)(2,1)}) %reduce-scatter.2.cloned.1.call-update) | async-done | bytes 1179664 | tf_op jit(solution)/shard_map/reduce_scatter | solution.py:74
  419.6 3.4 copy.95
  423.0 9.7 %all-to-all-start.1 = ((bf16[32,3,6144]{2,1,0:T(4,128)(2,1)}), bf16[32,3,6144]{2,1,0:T(4,128)(2,1)}, u32[]{:S(2)}, u32[]{:S(2)}) async-start(bf16[32,3,6144]{2,1,0:T(4,128)(2,1)} %copy.95), calls=%async_computation.2 | async-start | bytes 3145728 | tf_op jit(solution)/shard_map/all_to_all | solution.py:80
  432.9 36.7 %all-to-all-done.1 = bf16[32,3,6144]{2,1,0:T(4,128)(2,1)} async-done(((bf16[32,3,6144]{2,1,0:T(4,128)(2,1)}), bf16[32,3,6144]{2,1,0:T(4,128)(2,1)}, u32[]{:S(2)}, u32[]{:S(2)}) %all-to-all-start.1) | async-done | bytes 1179680 | tf_op jit(solution)/shard_map/all_to_all | solution.py:80
  469.6 2.4 convert_reduce_fusion
  472.0 0.4 fusion
  472.4 17.0 %all_to_all.16 = bf16[8,48,768]{2,1,0:T(8,128)(2,1)} all-to-all(bf16[8,48,768]{2,1,0:T(8,128)(2,1)S(1)} %bitcast.41), channel_id=1, replica_groups=mesh['section'=8,'ep'=32] {'section'}, dimensions={0} | all-to-all | bytes 1179648 | tf_op jit(solution)/shard_map/all_to_all | solution.py:32
  489.4 1.8 reduce_sum.55
  (25 shorter events, 0.8 us)
Async XLA Ops:
  6.5 322.5 %copy-start = (bf16[1,256,6144]{2,1,0:T(8,128)(2,1)S(1)}, bf16[1,256,6144]{2,1,0:T(8,128)(2,1)}, u32[]{:S(2)}) copy-start(bf16[1,256,6144]{2,1,0:T(8,128)(2,1)} %param.11) | copy-start | bytes 9437188
  6.5 413.0 %reduce-scatter.2.cloned.1.call-start = ((), (), s32[]{:S(2)}) async-start(), calls=%async_computation.4 | async-start | bytes 10616832 | tf_op jit(solution)/shard_map/reduce_scatter | solution.py:74
  67.9 1.2 copy-start.1
  69.9 18.0 %collective-permute-start = (bf16[32,3,6144]{2,0,1:T(8,128)(2,1)S(1)}, bf16[32,3,6144]{2,0,1:T(8,128)(2,1)S(1)}, u32[]{:S(2)}, u32[]{:S(2)}) collective-permute-start(bf16[32,3,6144]{2,0,1:T(8,128)(2,1)S(1)} %copy.85), channel_id=1, source_target_pairs={{0,32},{32,64},{64,96},{96,128},{128,160},{160,192},{192,224},{224... | collective-permute-start | bytes 3538952 | tf_op jit(solution)/shard_map/ppermute | solution.py:15
  74.8 15.6 %collective-permute-start.1 = (bf16[32,3,6144]{2,0,1:T(8,128)(2,1)S(1)}, bf16[32,3,6144]{2,0,1:T(8,128)(2,1)S(1)}, u32[]{:S(2)}, u32[]{:S(2)}) collective-permute-start(bf16[32,3,6144]{2,0,1:T(8,128)(2,1)S(1)} %copy.85), channel_id=1, source_target_pairs={{0,224},{32,0},{64,32},{96,64},{128,96},{160,128},{192,160},{224,1... | collective-permute-start | bytes 3538952 | tf_op jit(solution)/shard_map/ppermute | solution.py:18
  87.9 31.3 %copy-start.4 = (bf16[32,3,6144]{2,0,1:T(8,128)(2,1)}, bf16[32,3,6144]{2,0,1:T(8,128)(2,1)S(1)}, u32[]{:S(2)}) copy-start(bf16[32,3,6144]{2,0,1:T(8,128)(2,1)S(1)} %collective-permute-done) | copy-start | bytes 3538948
  87.9 15.6 %collective-permute-start.2 = (bf16[32,3,6144]{2,0,1:T(8,128)(2,1)S(1)}, bf16[32,3,6144]{2,0,1:T(8,128)(2,1)S(1)}, u32[]{:S(2)}, u32[]{:S(2)}) collective-permute-start(bf16[32,3,6144]{2,0,1:T(8,128)(2,1)S(1)} %collective-permute-done), channel_id=1, source_target_pairs={{0,32},{32,64},{64,96},{96,128},{128,160},{160,192},{192,224},{224... | collective-permute-start | bytes 3538952 | tf_op jit(solution)/shard_map/ppermute | solution.py:15
  90.4 1.0 copy-start.2
  91.5 15.7 %collective-permute-start.3 = (bf16[32,3,6144]{2,0,1:T(8,128)(2,1)S(1)}, bf16[32,3,6144]{2,0,1:T(8,128)(2,1)}, u32[]{:S(2)}, u32[]{:S(2)}) collective-permute-start(bf16[32,3,6144]{2,0,1:T(8,128)(2,1)S(1)} %collective-permute-done.1), channel_id=1, source_target_pairs={{0,224},{32,0},{64,32},{96,64},{128,96},{160,128},{192,160},{224,1... | collective-permute-start | bytes 3538952 | tf_op jit(solution)/shard_map/ppermute | solution.py:18
  103.6 3.6 copy-start.3
  103.6 15.6 %collective-permute-start.4 = (bf16[32,3,6144]{2,0,1:T(8,128)(2,1)S(1)}, bf16[32,3,6144]{2,0,1:T(8,128)(2,1)}, u32[]{:S(2)}, u32[]{:S(2)}) collective-permute-start(bf16[32,3,6144]{2,0,1:T(8,128)(2,1)S(1)} %collective-permute-done.2), channel_id=1, source_target_pairs={{0,32},{32,64},{64,96},{96,128},{128,160},{160,192},{192,224},{224... | collective-permute-start | bytes 3538952 | tf_op jit(solution)/shard_map/ppermute | solution.py:15
  107.2 163.8 %collective-permute-start.5 = (bf16[32,3,6144]{2,0,1:T(8,128)(2,1)}, bf16[32,3,6144]{2,0,1:T(8,128)(2,1)}, u32[]{:S(2)}, u32[]{:S(2)}) collective-permute-start(bf16[32,3,6144]{2,0,1:T(8,128)(2,1)} %collective-permute-done.3), channel_id=1, source_target_pairs={{0,224},{32,0},{64,32},{96,64},{128,96},{160,128},{192,160},{224,1... | collective-permute-start | bytes 3538952 | tf_op jit(solution)/shard_map/ppermute | solution.py:18
  119.2 176.7 %collective-permute-start.6 = (bf16[32,3,6144]{2,0,1:T(8,128)(2,1)}, bf16[32,3,6144]{2,0,1:T(8,128)(2,1)}, u32[]{:S(2)}, u32[]{:S(2)}) collective-permute-start(bf16[32,3,6144]{2,0,1:T(8,128)(2,1)} %collective-permute-done.4), channel_id=1, source_target_pairs={{0,32},{32,64},{64,96},{96,128},{128,160},{160,192},{192,224},{224... | collective-permute-start | bytes 3538952 | tf_op jit(solution)/shard_map/ppermute | solution.py:15
  360.9 71.8 %copy-start.5 = (f32[48,2]{0,1:T(2,128)S(1)}, f32[48,2]{0,1:T(2,128)}, u32[]{:S(2)}) copy-start(f32[48,2]{0,1:T(2,128)} %param.8) | copy-start | bytes 1156
  423.0 46.6 %all-to-all-start.1 = ((bf16[32,3,6144]{2,1,0:T(4,128)(2,1)}), bf16[32,3,6144]{2,1,0:T(4,128)(2,1)}, u32[]{:S(2)}, u32[]{:S(2)}) async-start(bf16[32,3,6144]{2,1,0:T(4,128)(2,1)} %copy.95), calls=%async_computation.2 | async-start | bytes 3145728 | tf_op jit(solution)/shard_map/all_to_all | solution.py:80
Sparse Core Ops, SparseCore 0:
  361.0 58.4 reduce-scatter.1
